TPU v7x, 32 devices: a whole 2x2x4 slice. The times are simulated.
32 devices in a mesh: batch: 2 (over y), space: 8 (over z, x), hidden: 2 (over core).
Axes of the slice: x: 2, y: 2, z: 4, core: 2. Of those that a mesh axis runs over, the one named last changes fastest.
Arguments:
- nodes: bfloat16 [2, 1024, 512], P('batch', 'space'), may hold values from -6 to 6
- edges: bfloat16 [2, 8192, 512], P('batch', 'space'), may hold values from -6 to 6
- node_cotangent: bfloat16 [2, 1024, 512], P('batch', 'space'), may hold values from -18 to 18
- edge_cotangent: bfloat16 [2, 8192, 512], P('batch', 'space'), may hold values from -18 to 18
- senders: int32 [8192], P('space'), may hold values from 0 to 255
- receivers: int32 [8192], P('space'), may hold values from 0 to 127
- send_lists: int32 [8, 2, 64], P('space'), may hold values from 0 to 127
- edge_first: bfloat16 [1536, 512], P(None, 'hidden'), may hold values from -0.15625 to 0.15625
- edge_bias: float32 [512], P('hidden'), may hold values from -3 to 3
- edge_second: bfloat16 [512, 512], P('hidden'), may hold values from -0.25 to 0.25
- edge_gain: float32 [512], replicated, may hold values from 0.1 to 1.9
- node_first: bfloat16 [1024, 512], replicated, may hold values from -0.1875 to 0.1875
- node_bias: float32 [512], replicated, may hold values from -3 to 3
- node_second: bfloat16 [512, 512], replicated, may hold values from -0.25 to 0.25
- node_gain: float32 [512], replicated, may hold values from 0.1 to 1.9
Outputs:
- grad_nodes: bfloat16 [2, 1024, 512], P('batch', 'space', 'hidden')
- grad_edges: bfloat16 [2, 8192, 512], P('batch', 'space', 'hidden')
- grad_edge_first: float32 [1536, 512], P(None, 'hidden')
- grad_edge_bias: float32 [512], P('hidden')
- grad_edge_second: float32 [512, 512], P('hidden')
- grad_edge_gain: float32 [512], replicated
- grad_node_first: float32 [1024, 512], replicated
- grad_node_bias: float32 [512], replicated
- grad_node_second: float32 [512, 512], replicated
- grad_node_gain: float32 [512], replicated
Inputs may be any that keep to these rules, and one draw needn't show every extreme that they name: `senders`: an entry below 128 is a local node of the edge's patch; 128 + k is row k of the previous patch's list 1, 192 + k row k of the next patch's list 0. `receivers`: local nodes of the edge's patch. `send_lists`: local nodes of the patch; entries may repeat.
All inputs are finite; a program needn't handle non-finite values.
Results may differ from a plain program's by a relative error of at most 0.015.
Values may be sent and summed in bfloat16 or wider, within the bound.
A program may use at most 128 MiB of HBM per device.

v0:
```python
import jax
import jax.numpy as jnp
from jax import lax
from jax.sharding import PartitionSpec as P

EPS = 1e-05


def extended(cells, sides, width):
    for axis, dim in sides:
        count = lax.axis_size(axis)
        head = lax.slice_in_dim(cells, 0, width, axis=dim)
        tail = lax.slice_in_dim(cells, cells.shape[dim] - width, cells.shape[dim], axis=dim)
        cells = jnp.concatenate(
            [
                lax.ppermute(tail, axis, [(i, (i + 1) % count) for i in range(count)]),
                cells,
                lax.ppermute(head, axis, [((i + 1) % count, i) for i in range(count)]),
            ],
            axis=dim,
        )
    return cells


def one_hot(indices, columns, wanted):
    return (indices[:, None] == jnp.arange(columns, dtype=jnp.int32)[None, :]).astype(wanted)


def matmul(lefthand, righthand):
    return jnp.dot(lefthand, righthand, preferred_element_type=jnp.float32)


def matmul_tn(lefthand, righthand):
    return lax.dot_general(
        lefthand, righthand, (((0,), (0,)), ((), ())), preferred_element_type=jnp.float32
    )


def matmul_nt(lefthand, righthand):
    return lax.dot_general(
        lefthand, righthand, (((1,), (1,)), ((), ())), preferred_element_type=jnp.float32
    )


def exact_tn(lefthand, righthand):
    return lax.dot_general(
        lefthand,
        righthand,
        (((0,), (0,)), ((), ())),
        precision=lax.Precision.HIGHEST,
        preferred_element_type=jnp.float32,
    )


def normalize(values):
    centre = values - jnp.mean(values, axis=-1, keepdims=True)
    scaled = lax.rsqrt(jnp.mean(centre * centre, axis=-1, keepdims=True) + EPS)
    return (centre * scaled, scaled)


def norm_back(upstream, gain_vec, normed, scaled):
    pulled = upstream * gain_vec
    return scaled * (
        pulled
        - jnp.mean(pulled, axis=-1, keepdims=True)
        - normed * jnp.mean(pulled * normed, axis=-1, keepdims=True)
    )


def silu_slope(values):
    logistic = jax.nn.sigmoid(values)
    return logistic * (1.0 + values * (1.0 - logistic))


def on_device(
    nodes,
    edges,
    node_cotangent,
    edge_cotangent,
    senders,
    receivers,
    send_lists,
    edge_first,
    edge_bias,
    edge_second,
    edge_gain,
    node_first,
    node_bias,
    node_second,
    node_gain,
):
    splits = lax.axis_size("hidden")
    my_part = lax.axis_index("hidden")
    width = nodes.shape[2]
    half = width // splits
    node_rows = nodes[0]
    node_count = node_rows.shape[0]
    halo_count = send_lists.shape[2]
    listed = send_lists[0].reshape(-1)
    picker = one_hot(listed, node_count, jnp.bfloat16)
    outgoing = matmul(picker, node_rows).astype(jnp.bfloat16).reshape(2, halo_count, width)
    padded = extended(outgoing, (("space", 0),), 1)
    table = jnp.concatenate([node_rows, padded[0], padded[3]], axis=0)
    table_rows = table.shape[0]
    sender_hot = one_hot(senders, table_rows, jnp.bfloat16)
    receiver_hot = one_hot(receivers, node_count, jnp.bfloat16)
    from_sender = matmul(sender_hot, table).astype(jnp.bfloat16)
    from_receiver = matmul(receiver_hot, node_rows).astype(jnp.bfloat16)
    edge_input = jnp.concatenate([edges[0], from_sender, from_receiver], axis=1)
    edge_pre = matmul(edge_input, edge_first) + edge_bias
    edge_act = jax.nn.silu(edge_pre).astype(jnp.bfloat16)
    edge_total = lax.psum(matmul(edge_act, edge_second).astype(jnp.bfloat16), "hidden").astype(
        jnp.float32
    )
    edge_normed, edge_scale = normalize(edge_total)
    message = (edge_gain * edge_normed).astype(jnp.bfloat16)
    gathered = matmul_tn(receiver_hot, message).astype(jnp.bfloat16)
    node_input = jnp.concatenate([node_rows, gathered], axis=1)
    node_pre = matmul(node_input, node_first) + node_bias
    node_act = jax.nn.silu(node_pre).astype(jnp.bfloat16)
    node_normed, node_scale = normalize(matmul(node_act, node_second))
    node_upstream = node_cotangent[0].astype(jnp.float32)
    node_gain_grad = jnp.sum(node_upstream * node_normed, axis=0)
    node_dz = norm_back(node_upstream, node_gain, node_normed, node_scale).astype(jnp.bfloat16)
    node_second_grad = matmul_tn(node_act, node_dz)
    node_dh = (matmul_nt(node_dz, node_second) * silu_slope(node_pre)).astype(jnp.bfloat16)
    node_first_grad = matmul_tn(node_input, node_dh)
    node_bias_grad = jnp.sum(node_dh.astype(jnp.float32), axis=0)
    node_dx = matmul_nt(node_dh, node_first)
    agg_grad = node_dx[:, width:].astype(jnp.bfloat16)
    edge_upstream = edge_cotangent[0].astype(jnp.float32)
    message_grad = edge_upstream + matmul(receiver_hot, agg_grad)
    edge_gain_grad = jnp.sum(message_grad * edge_normed, axis=0)
    edge_dz = norm_back(message_grad, edge_gain, edge_normed, edge_scale).astype(jnp.bfloat16)
    edge_second_grad = matmul_tn(edge_act, edge_dz)
    edge_dh = (matmul_nt(edge_dz, edge_second) * silu_slope(edge_pre)).astype(jnp.bfloat16)
    edge_first_grad = matmul_tn(edge_input, edge_dh)
    edge_bias_grad = jnp.sum(edge_dh.astype(jnp.float32), axis=0)
    sender_exact = one_hot(senders, table_rows, jnp.float32)
    receiver_exact = one_hot(receivers, node_count, jnp.float32)
    blocks = edge_first.reshape(3, splits, half, edge_first.shape[1])
    mine = lax.all_to_all(blocks, "hidden", split_axis=1, concat_axis=3, tiled=True).reshape(
        3 * half, -1
    )
    input_grad = matmul_nt(lax.all_gather(edge_dh, "hidden", axis=1, tiled=True), mine)
    edge_own = input_grad[:, :half]
    sender_grad = exact_tn(sender_exact, input_grad[:, half : 2 * half])
    receiver_grad = exact_tn(receiver_exact, input_grad[:, 2 * half :])
    table_grad = jnp.concatenate(
        [sender_grad[:node_count] + receiver_grad, sender_grad[node_count:]], axis=0
    )
    returning = jnp.stack(
        [table_grad[node_count : node_count + halo_count], table_grad[node_count + halo_count :]],
        axis=0,
    )
    returned = extended(returning.astype(jnp.bfloat16), (("space", 0),), 1).astype(returning.dtype)
    arriving = jnp.concatenate([returned[0], returned[3]], axis=0)
    halo_grad = exact_tn(one_hot(listed, node_count, jnp.float32), arriving)
    own_cot = lax.dynamic_slice_in_dim(node_upstream, my_part * half, half, 1)
    own_node = lax.dynamic_slice_in_dim(node_dx, my_part * half, half, 1)
    grad_nodes = (own_cot + own_node + table_grad[:node_count] + halo_grad).astype(jnp.bfloat16)[
        None
    ]
    own_edge_cot = lax.dynamic_slice_in_dim(edge_upstream, my_part * half, half, 1)
    grad_edges = (own_edge_cot + edge_own).astype(jnp.bfloat16)[None]
    (
        edge_first_grad,
        edge_bias_grad,
        edge_second_grad,
        edge_gain_grad,
        node_first_grad,
        node_bias_grad,
        node_second_grad,
        node_gain_grad,
    ) = lax.psum(
        (
            edge_first_grad,
            edge_bias_grad,
            edge_second_grad,
            edge_gain_grad,
            node_first_grad,
            node_bias_grad,
            node_second_grad,
            node_gain_grad,
        ),
        ("batch", "space"),
    )
    return (
        grad_nodes,
        grad_edges,
        edge_first_grad,
        edge_bias_grad,
        edge_second_grad,
        edge_gain_grad,
        node_first_grad,
        node_bias_grad,
        node_second_grad,
        node_gain_grad,
    )


def solution(mesh):
    placed = (
        P("batch", "space", None),
        P("batch", "space", None),
        P("batch", "space", None),
        P("batch", "space", None),
        P("space"),
        P("space"),
        P("space", None, None),
        P(None, "hidden"),
        P("hidden"),
        P("hidden", None),
        P(),
        P(),
        P(),
        P(),
        P(),
    )
    return jax.shard_map(
        on_device,
        mesh=mesh,
        in_specs=placed,
        out_specs=(
            P("batch", "space", "hidden"),
            P("batch", "space", "hidden"),
            P(None, "hidden"),
            P("hidden"),
            P("hidden", None),
            P(),
            P(),
            P(),
            P(),
            P(),
        ),
        check_vma=False,
    )
```

profile of v0, /device:TPU:0, one launch (start us, length us, event | category | flops | bytes accessed | tf_op | source)
XLA Modules:
  0.0 280.4 jit_solution(7566066074686124205)
XLA Ops:
  8.7 1.1 convolution_convert_fusion.4
  9.8 3.0 %collective-permute-start = (bf16[1,64,512]{2,1,0:T(8,128)(2,1)S(1)}, bf16[1,64,512]{2,1,0:T(8,128)(2,1)S(1)}, u32[]{:S(2)}, u32[]{:S(2)}) collective-permute-start(bf16[1,64,512]{2,1,0:T(8,128)(2,1)S(1)} %get-tuple-element.28), channel_id=1, source_target_pairs={{0,2},{2,4},{4,6},{6,8},{8,10},{10,12},{12,14},{14,0},{1,3},{3,5},... | collective-permute-start | bytes 196616 | tf_op jit(solution)/shard_map/ppermute | solution.py:16
  12.9 3.1 %collective-permute-start.1 = (bf16[1,64,512]{2,1,0:T(8,128)(2,1)S(1)}, bf16[1,64,512]{2,1,0:T(8,128)(2,1)S(1)}, u32[]{:S(2)}, u32[]{:S(2)}) collective-permute-start(bf16[1,64,512]{2,1,0:T(8,128)(2,1)S(1)} %get-tuple-element.29), channel_id=1, source_target_pairs={{2,0},{4,2},{6,4},{8,6},{10,8},{12,10},{14,12},{0,14},{3,1},{5,3},... | collective-permute-start | bytes 196616 | tf_op jit(solution)/shard_map/ppermute | solution.py:18
  16.0 1.5 convolution_convert_fusion.2
  17.5 1.3 copy.33
  19.4 2.9 %convolution_add_fusion = f32[1024,256]{1,0:T(8,128)S(1)} fusion(bf16[1536,256]{1,0:T(8,128)(2,1)} %param.22, bf16[1024,512]{0,1:T(8,128)(2,1)S(1)} %convolution_convert_fusion.2, bf16[1024,512]{0,1:T(8,128)(2,1)S(1)} %convolution_convert_fusion, bf16[1024,512]{0,1:T(8,128)(2,1)} %bitcast.76, f32[256]{0:T(256)S(1)} %copy-done.35), kind=kOutput, calls=%fused_computation.22 | convolution fusion | flops 815005696 | bytes 4981760 | tf_op jit(solution)/shard_map/dot_general | solution.py:30
  22.3 1.4 convolution_convert_fusion.1
  23.8 20.5 %all-reduce.5.cloned.1.call-done = bf16[1024,512]{1,0:T(8,128)(2,1)} async-done(((bf16[1024,512]{1,0:T(8,128)(2,1)}), bf16[1024,512]{1,0:T(8,128)(2,1)}) %all-reduce.5.cloned.1.call-update) | async-done | bytes 1048592 | tf_op jit(solution)/shard_map/psum | solution.py:112
  44.4 1.5 convert_reduce_fusion
  45.9 1.7 fusion.12
  51.9 1.9 fusion.11
  55.1 1.9 convert_reduce_fusion.1
  57.1 2.5 fusion.55
  59.6 2.7 fusion.41
  62.4 1.3 fusion.57
  64.3 2.1 fusion.14
  66.4 1.1 copy-done.9
  68.5 4.4 %all-to-all-start = ((bf16[3,2,256,256]{3,2,0,1:T(8,128)(2,1)}), bf16[3,2,256,256]{3,2,0,1:T(8,128)(2,1)}, u32[]{:S(2)}, u32[]{:S(2)}) async-start(bf16[3,2,256,256]{3,2,0,1:T(8,128)(2,1)} %copy.35), calls=%async_computation | async-start | bytes 1572864 | tf_op jit(solution)/shard_map/all_to_all | solution.py:142
  72.9 1.5 convert_element_type.87
  75.0 1.9 copy.36
  76.9 1.1 copy.38
  78.0 46.1 %all-reduce = (f32[256]{0:T(256)}, f32[512]{0:T(512)}, f32[512]{0:T(512)}, f32[512]{0:T(512)}) all-reduce(f32[256]{0:T(256)S(1)} %copy-done.28, f32[512]{0:T(512)S(1)} %copy-done.27, f32[512]{0:T(512)S(1)} %copy-done.26, f32[512]{0:T(512)S(1)} %get-tuple-element.13), channel_id=1, replica_groups=mesh['batch'=2,'space'=8,'hidden'=2] {'batch','space'}, use_global_device_ids=true, to_apply=%region_11.12 | all-reduce | flops 1792 | bytes 14336 | tf_op jit(solution)/shard_map/psum | solution.py:175
  124.1 2.5 fusion.61
  126.6 1.2 fusion.59
  127.9 4.7 %collective-permute-start.3 = (bf16[1,64,256]{2,1,0:T(8,128)(2,1)S(1)}, bf16[1,64,256]{2,1,0:T(8,128)(2,1)S(1)}, u32[]{:S(2)}, u32[]{:S(2)}) collective-permute-start(bf16[1,64,256]{2,1,0:T(8,128)(2,1)S(1)} %get-tuple-element.27), channel_id=1, source_target_pairs={{2,0},{4,2},{6,4},{8,6},{10,8},{12,10},{14,12},{0,14},{3,1},{5,3},... | collective-permute-start | bytes 98312 | tf_op jit(solution)/shard_map/ppermute | solution.py:18
  132.6 1.0 fusion.27
  133.5 1.7 fusion.16
  135.3 1.0 fusion.18
  136.3 131.0 %all-reduce.7.cloned.1.call-done = (f32[1536,256]{1,0:T(8,128)}, f32[256,512]{1,0:T(8,128)}, f32[1024,512]{1,0:T(8,128)}, f32[512,512]{1,0:T(8,128)}) async-done(((f32[1536,256]{1,0:T(8,128)}, f32[256,512]{1,0:T(8,128)}, f32[1024,512]{1,0:T(8,128)}, f32[512,512]{1,0:T(8,128)}), (f32[1536,256]{1,0:T(8,128)}, f32[256,512]{1,0:T(8,128)}, f32[1024,512]{1,0:T(8,128)}, ...) | async-done | bytes 5242896 | tf_op jit(solution)/shard_map/psum | solution.py:175
  267.3 2.8 copy.44
  270.9 1.3 copy.46
  272.9 1.0 copy.47
  (117 shorter events, 11.2 us)
Async XLA Ops:
  7.2 41.4 %copy-start = (bf16[1024,512]{1,0:T(8,128)(2,1)S(1)}, bf16[1024,512]{1,0:T(8,128)(2,1)}, u32[]{:S(2)}) copy-start(bf16[1024,512]{1,0:T(8,128)(2,1)} %param.26) | copy-start | bytes 3145732
  7.2 11.6 %copy-start.2 = (bf16[1,128,512]{2,1,0:T(8,128)(2,1)S(1)}, bf16[1,128,512]{2,1,0:T(8,128)(2,1)}, u32[]{:S(2)}) copy-start(bf16[1,128,512]{2,1,0:T(8,128)(2,1)} %param.15) | copy-start | bytes 393220
  7.2 10.2 %copy-start.5 = (bf16[1,1024,512]{2,1,0:T(8,128)(2,1)S(1)}, bf16[1,1024,512]{2,1,0:T(8,128)(2,1)}, u32[]{:S(2)}) copy-start(bf16[1,1024,512]{2,1,0:T(8,128)(2,1)} %param.16) | copy-start | bytes 3145732
  7.2 11.6 %copy-start.18 = (s32[1024]{0:T(1024)S(1)}, s32[1024]{0:T(1024)}, u32[]{:S(2)}) copy-start(s32[1024]{0:T(1024)} %param.19) | copy-start | bytes 12292
  7.2 37.1 %all-reduce.5.cloned.1.call-start = ((), (), s32[]{:S(2)}) async-start(), calls=%async_computation.1 | async-start | bytes 2097152 | tf_op jit(solution)/shard_map/psum | solution.py:112
  9.8 8.9 %collective-permute-start = (bf16[1,64,512]{2,1,0:T(8,128)(2,1)S(1)}, bf16[1,64,512]{2,1,0:T(8,128)(2,1)S(1)}, u32[]{:S(2)}, u32[]{:S(2)}) collective-permute-start(bf16[1,64,512]{2,1,0:T(8,128)(2,1)S(1)} %get-tuple-element.28), channel_id=1, source_target_pairs={{0,2},{2,4},{4,6},{6,8},{8,10},{10,12},{12,14},{14,0},{1,3},{3,5},... | collective-permute-start | bytes 196616 | tf_op jit(solution)/shard_map/ppermute | solution.py:16
  12.9 5.9 %collective-permute-start.1 = (bf16[1,64,512]{2,1,0:T(8,128)(2,1)S(1)}, bf16[1,64,512]{2,1,0:T(8,128)(2,1)S(1)}, u32[]{:S(2)}, u32[]{:S(2)}) collective-permute-start(bf16[1,64,512]{2,1,0:T(8,128)(2,1)S(1)} %get-tuple-element.29), channel_id=1, source_target_pairs={{2,0},{4,2},{6,4},{8,6},{10,8},{12,10},{14,12},{0,14},{3,1},{5,3},... | collective-permute-start | bytes 196616 | tf_op jit(solution)/shard_map/ppermute | solution.py:18
  19.4 2.9 %copy-start.36 = (bf16[1024,512]{0,1:T(8,128)(2,1)}, bf16[1024,512]{0,1:T(8,128)(2,1)S(1)}, u32[]{:S(2)}) copy-start(bf16[1024,512]{0,1:T(8,128)(2,1)S(1)} %convolution_convert_fusion) | copy-start | bytes 3145732
  19.4 2.9 %copy-start.33 = (bf16[256,512]{1,0:T(8,128)(2,1)S(1)}, bf16[256,512]{1,0:T(8,128)(2,1)}, u32[]{:S(2)}) copy-start(bf16[256,512]{1,0:T(8,128)(2,1)} %param.24) | copy-start | bytes 786436
  23.8 23.8 %copy-start.17 = (s32[1024]{0:T(1024)S(1)}, s32[1024]{0:T(1024)}, u32[]{:S(2)}) copy-start(s32[1024]{0:T(1024)} %param.20) | copy-start | bytes 12292
  23.8 23.8 %copy-start.20 = (f32[512]{0:T(512)S(1)}, f32[512]{0:T(512)}, u32[]{:S(2)}) copy-start(f32[512]{0:T(512)} %param.25) | copy-start | bytes 6148
  23.8 100.3 %all-gather.2.cloned.1.call-start = ((), (), s32[]{:S(2)}) async-start(), calls=%async_computation.2 | async-start | bytes 1572864 | tf_op jit(solution)/shard_map/all_gather | solution.py:145
  44.3 3.3 %copy-start.1 = (bf16[1024,512]{1,0:T(8,128)(2,1)S(1)}, bf16[1024,512]{1,0:T(8,128)(2,1)}, u32[]{:S(2)}) copy-start(bf16[1024,512]{1,0:T(8,128)(2,1)} %all-reduce.5.cloned.1.call-done) | copy-start | bytes 3145732
  45.9 2.7 copy-start.19
  48.5 2.2 copy-start.12
  49.5 2.3 copy-start.29
  49.8 2.1 copy-start.4
  49.8 4.0 %copy-start.30 = (f32[128]{0:T(128)}, f32[128]{0:T(128)S(1)}, u32[]{:S(2)}) copy-start(f32[128]{0:T(128)S(1)} %get-tuple-element.39) | copy-start | bytes 1540
  49.8 3.9 %copy-start.31 = (f32[128]{0:T(128)}, f32[128]{0:T(128)S(1)}, u32[]{:S(2)}) copy-start(f32[128]{0:T(128)S(1)} %get-tuple-element.40) | copy-start | bytes 1540
  55.1 2.0 copy-start.22
  57.0 210.2 %all-reduce.7.cloned.1.call-start = ((), (), s32[]{:S(2)}) async-start(), calls=%async_computation.3 | async-start | bytes 10485760 | tf_op jit(solution)/shard_map/psum | solution.py:175
  57.1 5.3 %copy-start.40 = (f32[1024,256]{1,0:T(8,128)S(1)}, f32[1024,256]{1,0:T(8,128)}, u32[]{:S(2)}) copy-start(f32[1024,256]{1,0:T(8,128)} %copy-done.38) | copy-start | bytes 3145732
  68.5 6.0 %copy-start.11 = (bf16[1,128,512]{2,1,0:T(8,128)(2,1)S(1)}, bf16[1,128,512]{2,1,0:T(8,128)(2,1)}, u32[]{:S(2)}) copy-start(bf16[1,128,512]{2,1,0:T(8,128)(2,1)} %param.17) | copy-start | bytes 393220
  68.5 6.5 %all-to-all-start = ((bf16[3,2,256,256]{3,2,0,1:T(8,128)(2,1)}), bf16[3,2,256,256]{3,2,0,1:T(8,128)(2,1)}, u32[]{:S(2)}, u32[]{:S(2)}) async-start(bf16[3,2,256,256]{3,2,0,1:T(8,128)(2,1)} %copy.35), calls=%async_computation | async-start | bytes 1572864 | tf_op jit(solution)/shard_map/all_to_all | solution.py:142
  74.5 3.5 %copy-start.26 = (f32[512]{0:T(512)S(1)}, f32[512]{0:T(512)}, u32[]{:S(2)}) copy-start(f32[512]{0:T(512)} %get-tuple-element.37) | copy-start | bytes 6148
  74.5 3.5 %copy-start.27 = (f32[512]{0:T(512)S(1)}, f32[512]{0:T(512)}, u32[]{:S(2)}) copy-start(f32[512]{0:T(512)} %get-tuple-element.10) | copy-start | bytes 6148
  74.5 3.5 %copy-start.28 = (f32[256]{0:T(256)S(1)}, f32[256]{0:T(256)}, u32[]{:S(2)}) copy-start(f32[256]{0:T(256)} %get-tuple-element.35) | copy-start | bytes 3076
  127.8 7.5 %collective-permute-start.2 = (bf16[1,64,256]{2,1,0:T(8,128)(2,1)S(1)}, bf16[1,64,256]{2,1,0:T(8,128)(2,1)S(1)}, u32[]{:S(2)}, u32[]{:S(2)}) collective-permute-start(bf16[1,64,256]{2,1,0:T(8,128)(2,1)S(1)} %get-tuple-element.26), channel_id=1, source_target_pairs={{0,2},{2,4},{4,6},{6,8},{8,10},{10,12},{12,14},{14,0},{1,3},{3,5},... | collective-permute-start | bytes 98312 | tf_op jit(solution)/shard_map/ppermute | solution.py:16
  127.9 7.4 %copy-start.24 = (s32[128]{0:T(128)S(1)}, s32[128]{0:T(128)}, u32[]{:S(2)}) copy-start(s32[128]{0:T(128)} %copy-done.23) | copy-start | bytes 1540
  127.9 7.4 %collective-permute-start.3 = (bf16[1,64,256]{2,1,0:T(8,128)(2,1)S(1)}, bf16[1,64,256]{2,1,0:T(8,128)(2,1)S(1)}, u32[]{:S(2)}, u32[]{:S(2)}) collective-permute-start(bf16[1,64,256]{2,1,0:T(8,128)(2,1)S(1)} %get-tuple-element.27), channel_id=1, source_target_pairs={{2,0},{4,2},{6,4},{8,6},{10,8},{12,10},{14,12},{0,14},{3,1},{5,3},... | collective-permute-start | bytes 98312 | tf_op jit(solution)/shard_map/ppermute | solution.py:18
  267.3 2.8 %copy-start.13 = (f32[256,512]{1,0:T(8,128)S(1)}, f32[256,512]{1,0:T(8,128)}, u32[]{:S(2)}) copy-start(f32[256,512]{1,0:T(8,128)} %get-tuple-element.45) | copy-start | bytes 1572868
  267.3 3.6 %copy-start.3 = (f32[1024,512]{1,0:T(8,128)S(1)}, f32[1024,512]{1,0:T(8,128)}, u32[]{:S(2)}) copy-start(f32[1024,512]{1,0:T(8,128)} %get-tuple-element.47) | copy-start | bytes 6291460
  (17 other events, 22.9 us)
Sparse Core Ops, SparseCore 0:
  23.9 20.3 all-reduce.4
  57.2 9.9 all-gather.1
  73.9 193.3 all-reduce.6
where the time goes:
time: 281 us; the launch traced here: 280 us
  waiting for transfers between devices  152 us (54%)
  blocking collectives  46.1 us (16%)
  matrix products  29.2 us (10%)
  local copies, waits for them, and re-layouts  16.2 us (6%)
  starting transfers between devices  15.4 us (5%)
  between operations  14.3 us (5%)
  other arithmetic  7.05 us (3%)
    psum x1, waiting for transfers between devices, on_device(): lax.psum((edge_first_grad, edge_bias_grad, edge_second_grad, edge_gain_gr...  131 us
    psum x1, blocking collectives, on_device(): lax.psum((edge_first_grad, edge_bias_grad, edge_second_grad, edge_gain_gr...  46.1 us
    psum x1, waiting for transfers between devices, on_device(): lax.psum(matmul(edge_act, edge_second).astype(jnp.bfloat16), 'hidden')  20.5 us
    unnamed x88, local copies, waits for them, and re-layouts  12.4 us
    dot_general x8, matrix products, matmul(): return jnp.dot(lefthand, righthand, preferred_element_type=jnp.float32)  9.97 us
    dot_general x5, matrix products, matmul_tn(): lax.dot_general(lefthand, righthand, (((0,), (0,)), ((), ())), preferred_...  9.58 us
    ppermute x2, starting transfers between devices, extended(): lax.ppermute(head, axis, [((i + 1) % count, i) for i in range(count)])  7.8 us
    dot_general x4, matrix products, matmul_nt(): lax.dot_general(lefthand, righthand, (((1,), (1,)), ((), ())), preferred_...  5.78 us
  transfers between devices with their start and end apart: 8, of which 3 were waited for; matrix products, arithmetic and copies ran while one was open for 9% of the time, Pallas kernels for 0%

commit v1 on v0

--- a/solution.py
+++ b/solution.py
@@ -2,6 +2,7 @@
 import jax.numpy as jnp
 from jax import lax
 from jax.sharding import PartitionSpec as P
+from jax.lax import psum
 
 EPS = 1e-05
 
@@ -172,18 +173,21 @@
         node_bias_grad,
         node_second_grad,
         node_gain_grad,
-    ) = lax.psum(
-        (
-            edge_first_grad,
-            edge_bias_grad,
-            edge_second_grad,
-            edge_gain_grad,
-            node_first_grad,
-            node_bias_grad,
-            node_second_grad,
-            node_gain_grad,
+    ) = psum(
+        psum(
+            (
+                edge_first_grad,
+                edge_bias_grad,
+                edge_second_grad,
+                edge_gain_grad,
+                node_first_grad,
+                node_bias_grad,
+                node_second_grad,
+                node_gain_grad,
+            ),
+            axis_name="space",
         ),
-        ("batch", "space"),
+        "batch",
     )
     return (
         grad_nodes,

time: 281 us -> 408 us (1.45)
  waiting for transfers between devices: 152 us -> 301 us
  blocking collectives: 46.1 us -> 25.5 us
    psum x1 -> x2, waiting for transfers between devices: 131 us -> 280 us  [the longest x1 184 us: on_device(): psum((edge_first_grad, edge_bias_grad, edge_second_grad, edge_gain_grad,...]
    psum x1 -> x2, blocking collectives: 46.1 us -> 25.5 us  [the longest x1 19.4 us: on_device(): psum((edge_first_grad, edge_bias_grad, edge_second_grad, edge_gain_grad,...]
    unnamed x88 -> x58, local copies, waits for them, and re-layouts: 12.4 us -> 11.4 us
  transfers between devices with their start and end apart: 8 -> 9, of which waited for: 3 -> 4; matrix products, arithmetic and copies ran while one was open for 9% -> 4% of each run, Pallas kernels for 0% -> 0%
where the time goes in v1:
time: 408 us; the launch traced here: 407 us
  waiting for transfers between devices  301 us (74%)
  matrix products  28.5 us (7%)
  blocking collectives  25.5 us (6%)
  starting transfers between devices  15.4 us (4%)
  local copies, waits for them, and re-layouts  15.3 us (4%)
  between operations  14.2 us (3%)
  other arithmetic  7.11 us (2%)
    psum x1, waiting for transfers between devices, on_device(): psum((edge_first_grad, edge_bias_grad, edge_second_grad, edge_gain_grad,...  184 us
    psum x1, waiting for transfers between devices, on_device(): psum(psum((edge_first_grad, edge_bias_grad, edge_second_grad, edge_gain_g...  95.3 us
    psum x1, waiting for transfers between devices, on_device(): lax.psum(matmul(edge_act, edge_second).astype(jnp.bfloat16), 'hidden')  20.5 us
    psum x1, blocking collectives, on_device(): psum((edge_first_grad, edge_bias_grad, edge_second_grad, edge_gain_grad,...  19.4 us
    unnamed x58, local copies, waits for them, and re-layouts  11.4 us
    dot_general x8, matrix products, matmul(): return jnp.dot(lefthand, righthand, preferred_element_type=jnp.float32)  9.99 us
    dot_general x5, matrix products, matmul_tn(): lax.dot_general(lefthand, righthand, (((0,), (0,)), ((), ())), preferred_...  8.89 us
  transfers between devices with their start and end apart: 9, of which 4 were waited for; matrix products, arithmetic and copies ran while one was open for 4% of the time, Pallas kernels for 0%

profile of v1, /device:TPU:0, one launch (start us, length us, event | category | flops | bytes accessed | tf_op | source)
XLA Modules:
  0.0 407.4 jit_solution(2829657583601995586)
XLA Ops:
  8.2 1.1 convolution_convert_fusion.4
  9.3 3.0 collective-permute-start
  12.3 3.1 collective-permute-start.1
  15.4 1.5 convolution_convert_fusion.2
  17.0 1.3 copy.33
  18.9 2.9 convolution_add_fusion
  22.8 1.4 convolution_convert_fusion.1
  24.3 20.5 %all-reduce.8.cloned.1.call-done = bf16[1024,512]{1,0:T(8,128)(2,1)} async-done(((bf16[1024,512]{1,0:T(8,128)(2,1)}), bf16[1024,512]{1,0:T(8,128)(2,1)}) %all-reduce.8.cloned.1.call-update) | async-done | bytes 1048592 | tf_op jit(solution)/shard_map/psum | solution.py:113
  44.8 1.5 convert_reduce_fusion
  46.3 1.7 fusion.12
  51.1 1.5 fusion.55
  53.0 1.9 fusion.11
  56.1 1.9 convert_reduce_fusion.1
  58.0 1.3 fusion.57
  59.3 1.8 fusion.41
  61.1 3.5 fusion.14
  65.4 184.5 %all-reduce.10.cloned.1.call-done = (f32[1536,256]{1,0:T(8,128)}, f32[256,512]{1,0:T(8,128)}, f32[1024,512]{1,0:T(8,128)}, f32[512,512]{1,0:T(8,128)}) async-done(((f32[1536,256]{1,0:T(8,128)}, f32[256,512]{1,0:T(8,128)}, f32[1024,512]{1,0:T(8,128)}, f32[512,512]{1,0:T(8,128)}), (f32[1536,256]{1,0:T(8,128)}, f32[256,512]{1,0:T(8,128)}, f32[1024,512]{1,0:T(8,128)}, ...) | async-done | bytes 5242896 | tf_op jit(solution)/shard_map/psum | solution.py:177
  249.9 1.1 copy-done.9
  251.9 4.3 %all-to-all-start = ((bf16[3,2,256,256]{3,2,0,1:T(8,128)(2,1)}), bf16[3,2,256,256]{3,2,0,1:T(8,128)(2,1)}, u32[]{:S(2)}, u32[]{:S(2)}) async-start(bf16[3,2,256,256]{3,2,0,1:T(8,128)(2,1)} %copy.35), calls=%async_computation | async-start | bytes 1572864 | tf_op jit(solution)/shard_map/all_to_all | solution.py:143
  256.3 1.6 convert_element_type.87
  258.3 2.0 copy.36
  260.3 1.1 copy.38
  261.4 19.4 %all-reduce = (f32[256]{0:T(256)S(1)}, f32[512]{0:T(512)S(1)}, f32[512]{0:T(512)S(1)}, f32[512]{0:T(512)S(1)}) all-reduce(f32[256]{0:T(256)S(1)} %copy-done.19, f32[512]{0:T(512)S(1)} %copy-done.18, f32[512]{0:T(512)S(1)} %copy-done.17, f32[512]{0:T(512)S(1)} %get-tuple-element.13), channel_id=1, replica_groups=mesh['batch'=2,'space'=8,'hidden'=2] {'space'}, use_global_device_ids=true, to_apply=%region_12.13 | all-reduce | flops 1792 | bytes 14336 | tf_op jit(solution)/shard_map/psum | solution.py:177
  280.8 6.1 %all-reduce.2 = (f32[256]{0:T(256)}, f32[512]{0:T(512)}, f32[512]{0:T(512)}, f32[512]{0:T(512)}) all-reduce(f32[256]{0:T(256)S(1)} %get-tuple-element.16, f32[512]{0:T(512)S(1)} %get-tuple-element.17, f32[512]{0:T(512)S(1)} %get-tuple-element.18, f32[512]{0:T(512)S(1)} %get-tuple-element.19), channel_id=1, replica_groups=mesh['batch'=2,'space'=8,'hidden'=2] {'batch'}, use_global_device_ids=true, to_apply=%region_13.14 | all-reduce | flops 1792 | bytes 14336 | tf_op jit(solution)/shard_map/psum | solution.py:176
  286.9 2.5 fusion.61
  289.4 1.2 fusion.59
  290.7 4.7 %collective-permute-start.3 = (bf16[1,64,256]{2,1,0:T(8,128)(2,1)S(1)}, bf16[1,64,256]{2,1,0:T(8,128)(2,1)S(1)}, u32[]{:S(2)}, u32[]{:S(2)}) collective-permute-start(bf16[1,64,256]{2,1,0:T(8,128)(2,1)S(1)} %get-tuple-element.35), channel_id=1, source_target_pairs={{2,0},{4,2},{6,4},{8,6},{10,8},{12,10},{14,12},{0,14},{3,1},{5,3},... | collective-permute-start | bytes 98312 | tf_op jit(solution)/shard_map/ppermute | solution.py:19
  296.4 1.7 fusion.16
  299.0 95.3 %all-reduce.12.cloned.1.call-done = (f32[1536,256]{1,0:T(8,128)}, f32[256,512]{1,0:T(8,128)}, f32[1024,512]{1,0:T(8,128)}, f32[512,512]{1,0:T(8,128)}) async-done(((f32[1536,256]{1,0:T(8,128)}, f32[256,512]{1,0:T(8,128)}, f32[1024,512]{1,0:T(8,128)}, f32[512,512]{1,0:T(8,128)}), (f32[1536,256]{1,0:T(8,128)}, f32[256,512]{1,0:T(8,128)}, f32[1024,512]{1,0:T(8,128)}, ...) | async-done | bytes 5242896 | tf_op jit(solution)/shard_map/psum | solution.py:176
  394.3 2.8 copy.48
  397.9 1.3 copy.50
  399.9 1.0 copy.51
  (91 shorter events, 12.9 us)
Async XLA Ops:
  7.2 41.8 %copy-start = (bf16[1024,512]{1,0:T(8,128)(2,1)S(1)}, bf16[1024,512]{1,0:T(8,128)(2,1)}, u32[]{:S(2)}) copy-start(bf16[1024,512]{1,0:T(8,128)(2,1)} %param.26) | copy-start | bytes 3145732
  7.2 11.1 %copy-start.2 = (bf16[1,128,512]{2,1,0:T(8,128)(2,1)S(1)}, bf16[1,128,512]{2,1,0:T(8,128)(2,1)}, u32[]{:S(2)}) copy-start(bf16[1,128,512]{2,1,0:T(8,128)(2,1)} %param.15) | copy-start | bytes 393220
  7.2 9.7 %copy-start.5 = (bf16[1,1024,512]{2,1,0:T(8,128)(2,1)S(1)}, bf16[1,1024,512]{2,1,0:T(8,128)(2,1)}, u32[]{:S(2)}) copy-start(bf16[1,1024,512]{2,1,0:T(8,128)(2,1)} %param.16) | copy-start | bytes 3145732
  7.2 11.1 %copy-start.13 = (s32[1024]{0:T(1024)S(1)}, s32[1024]{0:T(1024)}, u32[]{:S(2)}) copy-start(s32[1024]{0:T(1024)} %param.19) | copy-start | bytes 12292
  7.2 37.6 %all-reduce.8.cloned.1.call-start = ((), (), s32[]{:S(2)}) async-start(), calls=%async_computation.1 | async-start | bytes 2097152 | tf_op jit(solution)/shard_map/psum | solution.py:113
  9.3 9.0 %collective-permute-start = (bf16[1,64,512]{2,1,0:T(8,128)(2,1)S(1)}, bf16[1,64,512]{2,1,0:T(8,128)(2,1)S(1)}, u32[]{:S(2)}, u32[]{:S(2)}) collective-permute-start(bf16[1,64,512]{2,1,0:T(8,128)(2,1)S(1)} %get-tuple-element.36), channel_id=1, source_target_pairs={{0,2},{2,4},{4,6},{6,8},{8,10},{10,12},{12,14},{14,0},{1,3},{3,5},... | collective-permute-start | bytes 196616 | tf_op jit(solution)/shard_map/ppermute | solution.py:17
  12.3 5.9 %collective-permute-start.1 = (bf16[1,64,512]{2,1,0:T(8,128)(2,1)S(1)}, bf16[1,64,512]{2,1,0:T(8,128)(2,1)S(1)}, u32[]{:S(2)}, u32[]{:S(2)}) collective-permute-start(bf16[1,64,512]{2,1,0:T(8,128)(2,1)S(1)} %get-tuple-element.37), channel_id=1, source_target_pairs={{2,0},{4,2},{6,4},{8,6},{10,8},{12,10},{14,12},{0,14},{3,1},{5,3},... | collective-permute-start | bytes 196616 | tf_op jit(solution)/shard_map/ppermute | solution.py:19
  16.9 2.0 copy-start.22
  18.9 2.9 copy-start.23
  18.9 3.9 copy-start.21
  24.2 23.8 %copy-start.12 = (s32[1024]{0:T(1024)S(1)}, s32[1024]{0:T(1024)}, u32[]{:S(2)}) copy-start(s32[1024]{0:T(1024)} %param.20) | copy-start | bytes 12292
  24.2 23.8 %copy-start.16 = (f32[512]{0:T(512)S(1)}, f32[512]{0:T(512)}, u32[]{:S(2)}) copy-start(f32[512]{0:T(512)} %param.25) | copy-start | bytes 6148
  24.3 225.6 %all-reduce.10.cloned.1.call-start = ((), (), s32[]{:S(2)}) async-start(), calls=%async_computation.3 | async-start | bytes 10485760 | tf_op jit(solution)/shard_map/psum | solution.py:177
  44.8 3.3 copy-start.1
  46.3 2.7 copy-start.14
  48.1 1.3 copy-start.20
  51.1 1.9 copy-start.4
  53.0 1.9 copy-start.8
  54.9 1.2 copy-start.25
  59.3 1.8 copy-start.7
  64.6 222.3 %all-gather.2.cloned.1.call-start = ((), (), s32[]{:S(2)}) async-start(), calls=%async_computation.2 | async-start | bytes 1572864 | tf_op jit(solution)/shard_map/all_gather | solution.py:146
  65.4 328.9 %all-reduce.12.cloned.1.call-start = ((), (), s32[]{:S(2)}) async-start(), calls=%async_computation.4 | async-start | bytes 10485760 | tf_op jit(solution)/shard_map/psum | solution.py:176
  249.9 1.1 copy-start.9
  251.9 6.4 %all-to-all-start = ((bf16[3,2,256,256]{3,2,0,1:T(8,128)(2,1)}), bf16[3,2,256,256]{3,2,0,1:T(8,128)(2,1)}, u32[]{:S(2)}, u32[]{:S(2)}) async-start(bf16[3,2,256,256]{3,2,0,1:T(8,128)(2,1)} %copy.35), calls=%async_computation | async-start | bytes 1572864 | tf_op jit(solution)/shard_map/all_to_all | solution.py:143
  257.9 3.5 copy-start.17
  257.9 3.5 copy-start.18
  257.9 3.5 copy-start.19
  290.6 7.4 %collective-permute-start.2 = (bf16[1,64,256]{2,1,0:T(8,128)(2,1)S(1)}, bf16[1,64,256]{2,1,0:T(8,128)(2,1)S(1)}, u32[]{:S(2)}, u32[]{:S(2)}) collective-permute-start(bf16[1,64,256]{2,1,0:T(8,128)(2,1)S(1)} %get-tuple-element.34), channel_id=1, source_target_pairs={{0,2},{2,4},{4,6},{6,8},{8,10},{10,12},{12,14},{14,0},{1,3},{3,5},... | collective-permute-start | bytes 98312 | tf_op jit(solution)/shard_map/ppermute | solution.py:17
  290.7 7.4 %collective-permute-start.3 = (bf16[1,64,256]{2,1,0:T(8,128)(2,1)S(1)}, bf16[1,64,256]{2,1,0:T(8,128)(2,1)S(1)}, u32[]{:S(2)}, u32[]{:S(2)}) collective-permute-start(bf16[1,64,256]{2,1,0:T(8,128)(2,1)S(1)} %get-tuple-element.35), channel_id=1, source_target_pairs={{2,0},{4,2},{6,4},{8,6},{10,8},{12,10},{14,12},{0,14},{3,1},{5,3},... | collective-permute-start | bytes 98312 | tf_op jit(solution)/shard_map/ppermute | solution.py:19
  394.3 2.8 copy-start.11
  394.3 3.6 copy-start.3
  397.9 2.0 copy-start.6
  (3 other events, 2.8 us)
Sparse Core Ops, SparseCore 0:
  24.4 20.3 all-reduce.7
  64.7 185.0 all-reduce.9
  252.0 7.7 all-gather.1
  262.3 131.9 all-reduce.11
